TPU v7x, 256 devices: a whole 4x4x8 slice. The times are simulated.
256 devices in a mesh: grp: 16 (over z, core), sub: 16 (over x, y).
Axes of the slice: x: 4, y: 4, z: 8, core: 2. Of those that a mesh axis runs over, the one named last changes fastest.
Arguments:
- coarse_op: float32 [256, 64, 576], P(('grp', 'sub'))
- right_side: float32 [256, 64, 64], P(('grp', 'sub')), may hold values from -6 to 6
- owner_map: int32 [256], replicated, may hold values from 0 to 255, as said below
- neighbor_table: int32 [256, 8], replicated, may hold values from 0 to 255, as said below
Outputs:
- solution: float32 [256, 64, 64], P(('grp', 'sub'))
Inputs may be any that keep to these rules, and one draw needn't show every extreme that they name: `owner_map`: a permutation of 0 .. 255. `neighbor_table`: row t lists the neighbours of coarse site t on a periodic 4^4 lattice in the order +x, -x, +y, -y, +z, -z, +t, -t; lattice positions carry the site numbers in a permuted order.
All inputs are finite; a program needn't handle non-finite values.
Results may differ from a plain program's by a relative error of at most 0.0001.
Values sent between devices are 32-bit elements; how exact they have to be, the bound alone decides.
A program may use at most 64 MiB of HBM per device.

v0:
```python
import jax
import jax.numpy as jnp
from jax import lax
from jax.sharding import PartitionSpec as P

ITERS = 3


def from_everyone(array, axis):
    copies = jnp.broadcast_to(array, (lax.axis_size(axis), *array.shape))
    return lax.all_to_all(copies, axis, split_axis=0, concat_axis=0, tiled=True)


def laid_out(parts, dim):
    parts = jnp.moveaxis(parts, 0, dim)
    shape = parts.shape
    return parts.reshape(*shape[:dim], shape[dim] * shape[dim + 1], *shape[dim + 2 :])


def gathered_copies(array, axis, dim):
    parts = from_everyone(array, axis)
    return laid_out(parts, dim)


def over_copies(array, axis):
    return from_everyone(array, axis).sum(axis=0)


def inner_product(first, second):
    return jnp.sum(first * second, axis=(0, 1))


def per_device(coarse_op, right_side, owner_map, neighbor_table):
    n_sub = lax.axis_size("sub")
    n_grp = lax.axis_size("grp")
    per_dev = coarse_op.shape[0]
    dof_count = coarse_op.shape[1]
    site_count = owner_map.shape[0]
    site_ids = jnp.arange(site_count, dtype=jnp.int32)
    inverse = jnp.sum(
        jnp.where(owner_map[None, :] == site_ids[:, None], site_ids[None, :], 0), axis=1
    )
    link = inverse[neighbor_table[owner_map]]
    op_rows = lax.all_gather(coarse_op, "grp", axis=0, tiled=True)
    rhs_rows = lax.all_to_all(right_side, "grp", split_axis=2, concat_axis=0, tiled=True)

    def reduce_sum(values):
        return jax.tree.map(lambda part: over_copies(part, "sub"), values)

    row_count = op_rows.shape[0]
    local_rows = jnp.arange(row_count, dtype=jnp.int32)
    own_slots = (
        local_rows // per_dev * n_sub + lax.axis_index("sub")
    ) * per_dev + local_rows % per_dev
    target = link[own_slots]
    target_block = target // per_dev
    position = (target_block % n_sub * n_grp + target_block // n_sub) * per_dev + target % per_dev
    rhs_count = rhs_rows.shape[2]
    beta = jnp.sqrt(reduce_sum(inner_product(rhs_rows, rhs_rows)))
    krylov = [rhs_rows / beta]
    hess = jnp.zeros((ITERS + 1, ITERS, rhs_count), jnp.float32)
    for column in range(ITERS):
        apply_vector = krylov[column]
        piece = gathered_copies(apply_vector, "sub", 0)
        count = piece.shape[0]
        select = (position[:, :, None] == jnp.arange(count, dtype=jnp.int32)[None, None, :]).astype(
            jnp.float32
        )
        nearby = jnp.einsum("lkr,rab->lkab", select, piece, precision=lax.Precision.HIGHEST)
        stacked = jnp.concatenate([apply_vector[:, None], nearby], axis=1).reshape(
            row_count, 9 * dof_count, rhs_count
        )
        image = jnp.einsum("sac,scr->sar", op_rows, stacked, precision=lax.Precision.HIGHEST)
        totals = reduce_sum(
            tuple(
                [inner_product(vector, image) for vector in krylov] + [inner_product(image, image)]
            )
        )
        norm_sq = totals[-1]
        for index_i in range(column + 1):
            image = image - totals[index_i] * krylov[index_i]
            hess = hess.at[index_i, column].set(totals[index_i])
            norm_sq = norm_sq - totals[index_i] * totals[index_i]
        norm_value = jnp.sqrt(norm_sq)
        hess = hess.at[column + 1, column].set(norm_value)
        krylov.append(image / norm_value)
    gram_matrix = jnp.einsum("ijr,ikr->rjk", hess, hess, precision=lax.Precision.HIGHEST)
    projected = (beta[None, :] * hess[0]).T
    factor = jnp.linalg.cholesky(gram_matrix)
    halfway = jax.scipy.linalg.solve_triangular(factor, projected[..., None], lower=True)
    weights = jax.scipy.linalg.solve_triangular(factor, halfway, lower=True, trans=1)[..., 0]
    solution = jnp.zeros_like(rhs_rows)
    for column in range(ITERS):
        solution = solution + weights[:, column][None, None, :] * krylov[column]
    return lax.all_to_all(solution, "grp", split_axis=0, concat_axis=2, tiled=True)


def solution(mesh):
    placed = (P(("grp", "sub"), None, None), P(("grp", "sub"), None, None), P(), P())
    return jax.shard_map(
        per_device,
        mesh=mesh,
        in_specs=placed,
        out_specs=P(("grp", "sub"), None, None),
        check_vma=False,
    )
```

profile of v0, /device:TPU:1, one launch (start us, length us, event | category | flops | bytes accessed | tf_op | source)
XLA Modules:
  0.0 240.6 jit_solution(6348703550296950979)
XLA Ops:
  6.5 0.7 all-gather.2.cloned.1.call-update
  7.3 0.8 copy.94
  8.7 0.8 reduce.42
  9.4 0.7 reshape.567
  10.1 10.0 %all-to-all-start = ((f32[16,1,256]{2,1,0:T(1,128)}), f32[16,1,256]{2,1,0:T(1,128)S(1)}, u32[]{:S(2)}, u32[]{:S(2)}) async-start(f32[16,1,256]{2,1,0:T(1,128)} %reshape.567), calls=%async_computation | async-start | bytes 32768 | tf_op jit(solution)/shard_map/all_to_all | solution.py:45
  20.1 0.8 copy.96
  20.9 0.7 compare_select_fusion.1
  21.6 0.7 gather_fusion
  22.5 0.8 select_reduce_fusion
  23.3 4.1 %all-to-all-done = f32[16,1,256]{2,1,0:T(1,128)S(1)} async-done(((f32[16,1,256]{2,1,0:T(1,128)}), f32[16,1,256]{2,1,0:T(1,128)S(1)}, u32[]{:S(2)}, u32[]{:S(2)}) %all-to-all-start) | async-done | bytes 16416 | tf_op jit(solution)/shard_map/all_to_all | solution.py:45
  27.4 0.7 reduce.43
  28.4 0.6 broadcast_in_dim.48
  29.0 6.8 %all-to-all-start.1 = ((f32[16,1,4]{2,1,0:T(1,128)}), f32[16,1,4]{2,1,0:T(1,128)S(1)}, u32[]{:S(2)}, u32[]{:S(2)}) async-start(f32[16,1,4]{2,1,0:T(1,128)} %broadcast_in_dim.48), calls=%async_computation.1 | async-start | bytes 16384 | tf_op jit(solution)/shard_map/all_to_all | solution.py:11
  35.8 13.1 %gather_fusion.1 = s32[2048]{0:T(1024)S(1)} fusion(s32[256]{0:T(256)S(1)} %select_reduce_fusion, s32[2048]{0:T(1024)S(1)} %broadcast_clamp_fusion), kind=kCustom, calls=%fused_computation.1 | custom fusion | bytes 24576 | tf_op jit(solution)/shard_map/gather | solution.py:43
  49.8 1.0 reshape.569
  50.8 6.7 %all-to-all-start.2 = ((f32[16,1,4096]{2,1,0:T(1,128)}), f32[16,1,4096]{2,1,0:T(1,128)S(1)}, u32[]{:S(2)}, u32[]{:S(2)}) async-start(f32[16,1,4096]{2,1,0:T(1,128)} %reshape.569), calls=%async_computation.2 | async-start | bytes 524288 | tf_op jit(solution)/shard_map/all_to_all | solution.py:11
  57.6 7.3 %all-to-all-done.2 = f32[16,1,4096]{2,1,0:T(1,128)S(1)} async-done(((f32[16,1,4096]{2,1,0:T(1,128)}), f32[16,1,4096]{2,1,0:T(1,128)S(1)}, u32[]{:S(2)}, u32[]{:S(2)}) %all-to-all-start.2) | async-done | bytes 262176 | tf_op jit(solution)/shard_map/all_to_all | solution.py:11
  64.9 1.3 reduce.44
  67.1 4.5 %multiply_reduce_fusion.8 = (f32[4]{0:T(128)S(1)}, f32[4]{0:T(128)S(1)}, f32[16,64,4]{1,2,0:T(4,128)S(1)}) fusion(f32[16,64,4]{1,2,0:T(4,128)S(1)} %broadcast_divide_fusion.1, f32[16,576,4]{1,2,0:T(4,128)S(1)} %reshape.564, f32[16,64,576]{2,1,0:T(8,128)} %all-gather.2.cloned.1.call-done), kind=kOutput, calls=%fused_computation.31 | convolution fusion | flops 28327928 | bytes 2539552 | tf_op jit(solution)/shard_map/sac,scr->sar/dot_general | solution.py:73
  71.6 9.8 %all_to_all.111 = f32[16,1,4]{2,1,0:T(1,128)S(1)} all-to-all(f32[16,1,4]{2,1,0:T(1,128)S(1)} %broadcast_in_dim.90), channel_id=1, replica_groups=mesh['grp'=16,'sub'=16] {'sub'}, dimensions={0} | all-to-all | bytes 512 | tf_op jit(solution)/shard_map/all_to_all | solution.py:11
  81.4 0.6 broadcast_in_dim.91
  82.0 3.5 %all-to-all-start.4 = ((f32[16,1,4]{2,1,0:T(1,128)}), f32[16,1,4]{2,1,0:T(1,128)S(1)}, u32[]{:S(2)}, u32[]{:S(2)}) async-start(f32[16,1,4]{2,1,0:T(1,128)} %broadcast_in_dim.91), calls=%async_computation.4 | async-start | bytes 16384 | tf_op jit(solution)/shard_map/all_to_all | solution.py:11
  85.6 6.3 %all-to-all-done.4 = f32[16,1,4]{2,1,0:T(1,128)S(1)} async-done(((f32[16,1,4]{2,1,0:T(1,128)}), f32[16,1,4]{2,1,0:T(1,128)S(1)}, u32[]{:S(2)}, u32[]{:S(2)}) %all-to-all-start.4) | async-done | bytes 288 | tf_op jit(solution)/shard_map/all_to_all | solution.py:11
  92.0 1.0 reshape.571
  93.0 3.8 %all-to-all-start.5 = ((f32[16,1,4096]{2,1,0:T(1,128)}), f32[16,1,4096]{2,1,0:T(1,128)S(1)}, u32[]{:S(2)}, u32[]{:S(2)}) async-start(f32[16,1,4096]{2,1,0:T(1,128)} %reshape.571), calls=%async_computation.5 | async-start | bytes 524288 | tf_op jit(solution)/shard_map/all_to_all | solution.py:11
  96.9 0.7 and_reduce_fusion
  97.6 6.6 %all-to-all-done.5 = f32[16,1,4096]{2,1,0:T(1,128)S(1)} async-done(((f32[16,1,4096]{2,1,0:T(1,128)}), f32[16,1,4096]{2,1,0:T(1,128)S(1)}, u32[]{:S(2)}, u32[]{:S(2)}) %all-to-all-start.5) | async-done | bytes 262176 | tf_op jit(solution)/shard_map/all_to_all | solution.py:11
  104.1 1.3 reduce.45
  106.3 2.8 %multiply_reduce_fusion.6 = (f32[4]{0:T(128)S(1)}, f32[4]{0:T(128)S(1)}, f32[4]{0:T(128)S(1)}, f32[16,64,4]{1,2,0:T(4,128)S(1)}) fusion(f32[16,64,4]{1,2,0:T(4,128)S(1)} %broadcast_divide_fusion.1, f32[16,64,4]{1,2,0:T(4,128)S(1)} %subtract_divide_fusion.1, f32[16,576,4]{1,2,0:T(4,128)S(1)} %reshape.565, f32[16,64,576]{2,1,0:T(8,128)S(1)} %copy-done), kind=kOutput, calls=%fused_computation.28 | convolution fusion | flops 28336116 | bytes 2555952 | tf_op jit(solution)/shard_map/sac,scr->sar/dot_general | solution.py:73
  109.1 0.6 broadcast_in_dim.94
  109.7 3.5 %all-to-all-start.6 = ((f32[16,1,4]{2,1,0:T(1,128)}), f32[16,1,4]{2,1,0:T(1,128)S(1)}, u32[]{:S(2)}, u32[]{:S(2)}) async-start(f32[16,1,4]{2,1,0:T(1,128)} %broadcast_in_dim.94), calls=%async_computation.6 | async-start | bytes 16384 | tf_op jit(solution)/shard_map/all_to_all | solution.py:11
  113.2 0.6 fusion.30
  113.9 5.7 %all-to-all-done.6 = f32[16,1,4]{2,1,0:T(1,128)S(1)} async-done(((f32[16,1,4]{2,1,0:T(1,128)}), f32[16,1,4]{2,1,0:T(1,128)S(1)}, u32[]{:S(2)}, u32[]{:S(2)}) %all-to-all-start.6) | async-done | bytes 288 | tf_op jit(solution)/shard_map/all_to_all | solution.py:11
  119.5 0.6 broadcast_in_dim.95
  120.1 3.5 %all-to-all-start.7 = ((f32[16,1,4]{2,1,0:T(1,128)}), f32[16,1,4]{2,1,0:T(1,128)S(1)}, u32[]{:S(2)}, u32[]{:S(2)}) async-start(f32[16,1,4]{2,1,0:T(1,128)} %broadcast_in_dim.95), calls=%async_computation.7 | async-start | bytes 16384 | tf_op jit(solution)/shard_map/all_to_all | solution.py:11
  123.6 0.7 fusion.31
  124.3 5.6 %all-to-all-done.7 = f32[16,1,4]{2,1,0:T(1,128)S(1)} async-done(((f32[16,1,4]{2,1,0:T(1,128)}), f32[16,1,4]{2,1,0:T(1,128)S(1)}, u32[]{:S(2)}, u32[]{:S(2)}) %all-to-all-start.7) | async-done | bytes 288 | tf_op jit(solution)/shard_map/all_to_all | solution.py:11
  129.9 0.6 broadcast_in_dim.96
  130.5 3.7 %all-to-all-start.8 = ((f32[16,1,4]{2,1,0:T(1,128)}), f32[16,1,4]{2,1,0:T(1,128)S(1)}, u32[]{:S(2)}, u32[]{:S(2)}) async-start(f32[16,1,4]{2,1,0:T(1,128)} %broadcast_in_dim.96), calls=%async_computation.8 | async-start | bytes 16384 | tf_op jit(solution)/shard_map/all_to_all | solution.py:11
  134.7 5.7 %all-to-all-done.8 = f32[16,1,4]{2,1,0:T(1,128)S(1)} async-done(((f32[16,1,4]{2,1,0:T(1,128)}), f32[16,1,4]{2,1,0:T(1,128)S(1)}, u32[]{:S(2)}, u32[]{:S(2)}) %all-to-all-start.8) | async-done | bytes 288 | tf_op jit(solution)/shard_map/all_to_all | solution.py:11
  141.2 1.0 reshape.573
  142.2 3.5 %all-to-all-start.9 = ((f32[16,1,4096]{2,1,0:T(1,128)}), f32[16,1,4096]{2,1,0:T(1,128)S(1)}, u32[]{:S(2)}, u32[]{:S(2)}) async-start(f32[16,1,4096]{2,1,0:T(1,128)} %reshape.573), calls=%async_computation.9 | async-start | bytes 524288 | tf_op jit(solution)/shard_map/all_to_all | solution.py:11
  146.9 6.2 %all-to-all-done.9 = f32[16,1,4096]{2,1,0:T(1,128)S(1)} async-done(((f32[16,1,4096]{2,1,0:T(1,128)}), f32[16,1,4096]{2,1,0:T(1,128)S(1)}, u32[]{:S(2)}, u32[]{:S(2)}) %all-to-all-start.9) | async-done | bytes 262176 | tf_op jit(solution)/shard_map/all_to_all | solution.py:11
  153.0 1.3 reduce.46
  155.3 2.8 %multiply_reduce_fusion = (f32[4]{0:T(128)S(1)}, f32[4]{0:T(128)S(1)}, f32[4]{0:T(128)S(1)}, f32[4]{0:T(128)S(1)}) fusion(f32[16,64,4]{1,2,0:T(4,128)S(1)} %subtract_divide_fusion, f32[16,64,4]{1,2,0:T(4,128)S(1)} %subtract_divide_fusion.1, f32[16,64,4]{1,2,0:T(4,128)S(1)} %broadcast_divide_fusion.1, f32[16,576,4]{1,2,0:T(4,128)S(1)} %reshape.566, ...), kind=kOutput, calls=%fused_computation.21 | convolution fusion | flops 28344304 | bytes 2555968 | tf_op jit(solution)/shard_map/sac,scr->sar/dot_general | solution.py:73
  158.1 0.6 broadcast_in_dim.99
  158.7 3.5 %all-to-all-start.10 = ((f32[16,1,4]{2,1,0:T(1,128)}), f32[16,1,4]{2,1,0:T(1,128)S(1)}, u32[]{:S(2)}, u32[]{:S(2)}) async-start(f32[16,1,4]{2,1,0:T(1,128)} %broadcast_in_dim.99), calls=%async_computation.10 | async-start | bytes 16384 | tf_op jit(solution)/shard_map/all_to_all | solution.py:11
  162.2 6.2 %all-to-all-done.10 = f32[16,1,4]{2,1,0:T(1,128)S(1)} async-done(((f32[16,1,4]{2,1,0:T(1,128)}), f32[16,1,4]{2,1,0:T(1,128)S(1)}, u32[]{:S(2)}, u32[]{:S(2)}) %all-to-all-start.10) | async-done | bytes 288 | tf_op jit(solution)/shard_map/all_to_all | solution.py:11
  169.1 3.5 %all-to-all-start.11 = ((f32[16,1,4]{2,1,0:T(1,128)}), f32[16,1,4]{2,1,0:T(1,128)S(1)}, u32[]{:S(2)}, u32[]{:S(2)}) async-start(f32[16,1,4]{2,1,0:T(1,128)} %broadcast_in_dim.100), calls=%async_computation.11 | async-start | bytes 16384 | tf_op jit(solution)/shard_map/all_to_all | solution.py:11
  172.6 6.3 %all-to-all-done.11 = f32[16,1,4]{2,1,0:T(1,128)S(1)} async-done(((f32[16,1,4]{2,1,0:T(1,128)}), f32[16,1,4]{2,1,0:T(1,128)S(1)}, u32[]{:S(2)}, u32[]{:S(2)}) %all-to-all-start.11) | async-done | bytes 288 | tf_op jit(solution)/shard_map/all_to_all | solution.py:11
  178.8 0.6 broadcast_in_dim.101
  179.4 3.5 %all-to-all-start.12 = ((f32[16,1,4]{2,1,0:T(1,128)}), f32[16,1,4]{2,1,0:T(1,128)S(1)}, u32[]{:S(2)}, u32[]{:S(2)}) async-start(f32[16,1,4]{2,1,0:T(1,128)} %broadcast_in_dim.101), calls=%async_computation.12 | async-start | bytes 16384 | tf_op jit(solution)/shard_map/all_to_all | solution.py:11
  182.9 1.4 scatter.34
  184.4 4.9 %all-to-all-done.12 = f32[16,1,4]{2,1,0:T(1,128)S(1)} async-done(((f32[16,1,4]{2,1,0:T(1,128)}), f32[16,1,4]{2,1,0:T(1,128)S(1)}, u32[]{:S(2)}, u32[]{:S(2)}) %all-to-all-start.12) | async-done | bytes 288 | tf_op jit(solution)/shard_map/all_to_all | solution.py:11
  189.2 0.6 broadcast_in_dim.102
  189.8 3.5 %all-to-all-start.13 = ((f32[16,1,4]{2,1,0:T(1,128)}), f32[16,1,4]{2,1,0:T(1,128)S(1)}, u32[]{:S(2)}, u32[]{:S(2)}) async-start(f32[16,1,4]{2,1,0:T(1,128)} %broadcast_in_dim.102), calls=%async_computation.13 | async-start | bytes 16384 | tf_op jit(solution)/shard_map/all_to_all | solution.py:11
  193.5 6.2 %all-to-all-done.13 = f32[16,1,4]{2,1,0:T(1,128)S(1)} async-done(((f32[16,1,4]{2,1,0:T(1,128)}), f32[16,1,4]{2,1,0:T(1,128)S(1)}, u32[]{:S(2)}, u32[]{:S(2)}) %all-to-all-start.13) | async-done | bytes 288 | tf_op jit(solution)/shard_map/all_to_all | solution.py:11
  199.6 1.8 fusion.28
  201.5 1.3 scatter.39
  203.4 1.1 custom-call.11
  204.8 1.0 custom-call.12
  206.9 25.4 %all_to_all.112 = f32[16,1,256]{2,1,0:T(1,128)S(1)} all-to-all(f32[16,1,256]{2,1,0:T(1,128)S(1)} %reshape.575), channel_id=1, replica_groups=mesh['grp'=16,'sub'=16] {'grp'}, dimensions={0} | all-to-all | bytes 32768 | tf_op jit(solution)/shard_map/all_to_all | solution.py:95
  232.2 0.7 reduce.47
  233.0 0.7 copy.129
  (116 shorter events, 9.9 us)
Async XLA Ops:
  6.5 60.6 %all-gather.2.cloned.1.call-start = ((), (), s32[]{:S(2)}) async-start(), calls=%async_computation.15 | async-start | bytes 2785280 | tf_op jit(solution)/shard_map/all_gather | solution.py:44
  10.1 17.3 %all-to-all-start = ((f32[16,1,256]{2,1,0:T(1,128)}), f32[16,1,256]{2,1,0:T(1,128)S(1)}, u32[]{:S(2)}, u32[]{:S(2)}) async-start(f32[16,1,256]{2,1,0:T(1,128)} %reshape.567), calls=%async_computation | async-start | bytes 32768 | tf_op jit(solution)/shard_map/all_to_all | solution.py:45
  29.0 20.6 %all-to-all-start.1 = ((f32[16,1,4]{2,1,0:T(1,128)}), f32[16,1,4]{2,1,0:T(1,128)S(1)}, u32[]{:S(2)}, u32[]{:S(2)}) async-start(f32[16,1,4]{2,1,0:T(1,128)} %broadcast_in_dim.48), calls=%async_computation.1 | async-start | bytes 16384 | tf_op jit(solution)/shard_map/all_to_all | solution.py:11
  50.8 14.1 %all-to-all-start.2 = ((f32[16,1,4096]{2,1,0:T(1,128)}), f32[16,1,4096]{2,1,0:T(1,128)S(1)}, u32[]{:S(2)}, u32[]{:S(2)}) async-start(f32[16,1,4096]{2,1,0:T(1,128)} %reshape.569), calls=%async_computation.2 | async-start | bytes 524288 | tf_op jit(solution)/shard_map/all_to_all | solution.py:11
  67.1 29.8 %copy-start.12 = (s32[3]{0:T(128)S(1)}, s32[3]{0:T(128)}, u32[]{:S(2)}) copy-start(s32[3]{0:T(128)} %constant.391.clone.1) | copy-start | bytes 40
  82.0 9.8 %all-to-all-start.4 = ((f32[16,1,4]{2,1,0:T(1,128)}), f32[16,1,4]{2,1,0:T(1,128)S(1)}, u32[]{:S(2)}, u32[]{:S(2)}) async-start(f32[16,1,4]{2,1,0:T(1,128)} %broadcast_in_dim.91), calls=%async_computation.4 | async-start | bytes 16384 | tf_op jit(solution)/shard_map/all_to_all | solution.py:11
  85.5 12.0 %copy-start.3 = (f32[4]{0:T(128)}, f32[4]{0:T(128)S(1)}, u32[]{:S(2)}) copy-start(f32[4]{0:T(128)S(1)} %reduce_sum.199) | copy-start | bytes 52
  91.8 5.7 %copy-start.9 = (f32[4]{0:T(128)}, f32[4]{0:T(128)S(1)}, u32[]{:S(2)}) copy-start(f32[4]{0:T(128)S(1)} %reduce_sum.201) | copy-start | bytes 52
  93.0 13.3 %copy-start = (f32[16,64,576]{2,1,0:T(8,128)S(1)}, f32[16,64,576]{2,1,0:T(8,128)}, u32[]{:S(2)}) copy-start(f32[16,64,576]{2,1,0:T(8,128)} %all-gather.2.cloned.1.call-done) | copy-start | bytes 7077892
  93.0 11.1 %all-to-all-start.5 = ((f32[16,1,4096]{2,1,0:T(1,128)}), f32[16,1,4096]{2,1,0:T(1,128)S(1)}, u32[]{:S(2)}, u32[]{:S(2)}) async-start(f32[16,1,4096]{2,1,0:T(1,128)} %reshape.571), calls=%async_computation.5 | async-start | bytes 524288 | tf_op jit(solution)/shard_map/all_to_all | solution.py:11
  106.3 40.0 %copy-start.4 = (f32[4]{0:T(128)S(1)}, f32[4]{0:T(128)}, u32[]{:S(2)}) copy-start(f32[4]{0:T(128)} %copy-done.3) | copy-start | bytes 52
  106.3 40.0 %copy-start.10 = (f32[4]{0:T(128)S(1)}, f32[4]{0:T(128)}, u32[]{:S(2)}) copy-start(f32[4]{0:T(128)} %copy-done.9) | copy-start | bytes 52
  109.7 9.8 %all-to-all-start.6 = ((f32[16,1,4]{2,1,0:T(1,128)}), f32[16,1,4]{2,1,0:T(1,128)S(1)}, u32[]{:S(2)}, u32[]{:S(2)}) async-start(f32[16,1,4]{2,1,0:T(1,128)} %broadcast_in_dim.94), calls=%async_computation.6 | async-start | bytes 16384 | tf_op jit(solution)/shard_map/all_to_all | solution.py:11
  120.1 9.8 %all-to-all-start.7 = ((f32[16,1,4]{2,1,0:T(1,128)}), f32[16,1,4]{2,1,0:T(1,128)S(1)}, u32[]{:S(2)}, u32[]{:S(2)}) async-start(f32[16,1,4]{2,1,0:T(1,128)} %broadcast_in_dim.95), calls=%async_computation.7 | async-start | bytes 16384 | tf_op jit(solution)/shard_map/all_to_all | solution.py:11
  130.5 10.0 %all-to-all-start.8 = ((f32[16,1,4]{2,1,0:T(1,128)}), f32[16,1,4]{2,1,0:T(1,128)S(1)}, u32[]{:S(2)}, u32[]{:S(2)}) async-start(f32[16,1,4]{2,1,0:T(1,128)} %broadcast_in_dim.96), calls=%async_computation.8 | async-start | bytes 16384 | tf_op jit(solution)/shard_map/all_to_all | solution.py:11
  134.7 12.2 %copy-start.1 = (f32[4]{0:T(128)}, f32[4]{0:T(128)S(1)}, u32[]{:S(2)}) copy-start(f32[4]{0:T(128)S(1)} %reduce_sum.204) | copy-start | bytes 52
  140.5 0.5 copy-start.6
  142.2 10.8 %all-to-all-start.9 = ((f32[16,1,4096]{2,1,0:T(1,128)}), f32[16,1,4096]{2,1,0:T(1,128)S(1)}, u32[]{:S(2)}, u32[]{:S(2)}) async-start(f32[16,1,4096]{2,1,0:T(1,128)} %reshape.573), calls=%async_computation.9 | async-start | bytes 524288 | tf_op jit(solution)/shard_map/all_to_all | solution.py:11
  154.6 7.5 %copy-start.5 = (f32[4]{0:T(128)S(1)}, f32[4]{0:T(128)}, u32[]{:S(2)}) copy-start(f32[4]{0:T(128)} %copy-done.3) | copy-start | bytes 52
  154.6 7.6 %copy-start.11 = (f32[1,1,4]{2,1,0:T(1,128)S(1)}, f32[1,1,4]{2,1,0:T(1,128)}, u32[]{:S(2)}) copy-start(f32[1,1,4]{2,1,0:T(1,128)} %fusion.27) | copy-start | bytes 52
  154.6 17.9 %copy-start.2 = (f32[4]{0:T(128)S(1)}, f32[4]{0:T(128)}, u32[]{:S(2)}) copy-start(f32[4]{0:T(128)} %copy-done.1) | copy-start | bytes 52
  154.6 17.9 %copy-start.7 = (f32[4]{0:T(128)S(1)}, f32[4]{0:T(128)}, u32[]{:S(2)}) copy-start(f32[4]{0:T(128)} %copy-done.6) | copy-start | bytes 52
  154.7 49.9 %copy-start.13 = (pred[3,3]{1,0:T(4,128)(4,1)S(1)}, pred[3,3]{1,0:T(4,128)(4,1)}, u32[]{:S(2)}) copy-start(pred[3,3]{1,0:T(4,128)(4,1)} %iota_compare_fusion.2) | copy-start | bytes 31
  154.7 50.1 %copy-start.8 = (pred[3,3]{1,0:T(4,128)(4,1)S(1)}, pred[3,3]{1,0:T(4,128)(4,1)}, u32[]{:S(2)}) copy-start(pred[3,3]{1,0:T(4,128)(4,1)} %iota_compare_fusion.3) | copy-start | bytes 31
  158.7 9.8 %all-to-all-start.10 = ((f32[16,1,4]{2,1,0:T(1,128)}), f32[16,1,4]{2,1,0:T(1,128)S(1)}, u32[]{:S(2)}, u32[]{:S(2)}) async-start(f32[16,1,4]{2,1,0:T(1,128)} %broadcast_in_dim.99), calls=%async_computation.10 | async-start | bytes 16384 | tf_op jit(solution)/shard_map/all_to_all | solution.py:11
  169.1 9.8 %all-to-all-start.11 = ((f32[16,1,4]{2,1,0:T(1,128)}), f32[16,1,4]{2,1,0:T(1,128)S(1)}, u32[]{:S(2)}, u32[]{:S(2)}) async-start(f32[16,1,4]{2,1,0:T(1,128)} %broadcast_in_dim.100), calls=%async_computation.11 | async-start | bytes 16384 | tf_op jit(solution)/shard_map/all_to_all | solution.py:11
  179.4 9.8 %all-to-all-start.12 = ((f32[16,1,4]{2,1,0:T(1,128)}), f32[16,1,4]{2,1,0:T(1,128)S(1)}, u32[]{:S(2)}, u32[]{:S(2)}) async-start(f32[16,1,4]{2,1,0:T(1,128)} %broadcast_in_dim.101), calls=%async_computation.12 | async-start | bytes 16384 | tf_op jit(solution)/shard_map/all_to_all | solution.py:11
  189.8 9.8 %all-to-all-start.13 = ((f32[16,1,4]{2,1,0:T(1,128)}), f32[16,1,4]{2,1,0:T(1,128)S(1)}, u32[]{:S(2)}, u32[]{:S(2)}) async-start(f32[16,1,4]{2,1,0:T(1,128)} %broadcast_in_dim.102), calls=%async_computation.13 | async-start | bytes 16384 | tf_op jit(solution)/shard_map/all_to_all | solution.py:11
Sparse Core Ops, SparseCore 0:
  9.2 44.2 all-gather.1
where the time goes:
time: 242 us; the launch traced here: 241 us
  waiting for transfers between devices  71.7 us (30%)
  starting transfers between devices  58.7 us (24%)
  blocking collectives  35.2 us (15%)
  local copies, waits for them, and re-layouts  34.1 us (14%)
  other arithmetic  15.4 us (6%)
  between operations  14 us (6%)
  matrix products  11.5 us (5%)
    all_to_all x12, waiting for transfers between devices, from_everyone(): return lax.all_to_all(copies, axis, split_axis=0, concat_axis=0, tiled=True)  66.9 us
    all_to_all x12, starting transfers between devices, from_everyone(): return lax.all_to_all(copies, axis, split_axis=0, concat_axis=0, tiled=True)  48.7 us
    all_to_all x1, blocking collectives, per_device(): lax.all_to_all(solution, 'grp', split_axis=0, concat_axis=2, tiled=True)  25.4 us
    gather x3, local copies, waits for them, and re-layouts, per_device(): link = inverse[neighbor_table[owner_map]]  14 us
    dot_general x3, matrix products, per_device(): jnp.einsum('sac,scr->sar', op_rows, stacked, precision=lax.Precision.HIGH...  10.1 us
    all_to_all x1, starting transfers between devices, per_device(): lax.all_to_all(right_side, 'grp', split_axis=2, concat_axis=0, tiled=True)  9.97 us
    all_to_all x1, blocking collectives, from_everyone(): return lax.all_to_all(copies, axis, split_axis=0, concat_axis=0, tiled=True)  9.8 us
    unnamed x48, local copies, waits for them, and re-layouts  7.99 us
  transfers between devices with their start and end apart: 14, of which 12 were waited for; matrix products, arithmetic and copies ran while one was open for 13% of the time, Pallas kernels for 0%

commit v1 on v0

v1 whole, which is shorter than its diff:
```python
import jax
import jax.numpy as jnp
from jax import lax
from jax.experimental import pallas as pl
from jax.experimental.pallas import tpu as pltpu
from jax.sharding import PartitionSpec as P

MESH = pl.DeviceIdType.MESH
NZ, NX, NY = 8, 4, 4
CH = 4
F32, BF16, I32 = jnp.float32, jnp.bfloat16, jnp.int32


def split(value):
    high = value.astype(BF16)
    return high, (value - high.astype(F32)).astype(BF16)


def dot_nt(left, right):
    return lax.dot_general(left, right, (((1,), (1,)), ((), ())), preferred_element_type=F32)


def fold8(value):
    return value.reshape(value.shape[0] // 8, 8, value.shape[1]).sum(axis=0)


def kernel(
    op_hbm, b_ref, om_ref, nt_ref, out_ref,
    opv, opb, wh, wl, pb, bb, z0, z1, z2, w1, w2, dh, dl, hot, xp, acc, pd, sb, ob,
    rx, tx_up, tx_dn, tx_sib, ld_sem, b_tx, b_rx, z_tx, z_rx, s_tx, s_rx,
):
    grp, sub = lax.axis_index("grp"), lax.axis_index("sub")
    z, core = grp // 2, grp % 2
    x, y = sub // NY, sub % NY

    def in_grp(e, q):
        return (z + e) % NZ * 2 + (core + q) % 2

    peers_z = [(e, q) for e in range(NZ) for q in range(2) if (e, q) != (0, 0)]
    peers_p = [(dx, dy) for dx in range(NX) for dy in range(NY) if (dx, dy) != (0, 0)]

    def plane(dx, dy):
        return {"grp": grp, "sub": (x + dx) % NX * NY + (y + dy) % NY}

    load = pltpu.make_async_copy(op_hbm.at[0], opv, ld_sem)
    load.start()
    barrier = pltpu.get_barrier_semaphore()
    for e, q in peers_z:
        pl.semaphore_signal(barrier, inc=1, device_id={"grp": in_grp(e, q), "sub": sub}, device_id_type=MESH)
    for dx, dy in peers_p:
        pl.semaphore_signal(barrier, inc=1, device_id=plane(dx, dy), device_id_type=MESH)

    bt = b_ref[0].T
    for p in range(2):
        pb[:, p, :] = jnp.concatenate([bt[32 * p : 32 * p + 16], bt[32 * p + 16 : 32 * p + 32]], axis=1)
    load.wait()
    for c in range(CH):
        for m in range(4):
            opb[0, 0, c, 16 * m : 16 * m + 16, :] = opv[16 * c : 16 * c + 16, 128 * m : 128 * m + 128]
        opb[0, 0, c, 64:72, :] = jnp.concatenate(
            [opv[16 * c : 16 * c + 8, 512:576], opv[16 * c + 8 : 16 * c + 16, 512:576]], axis=1
        )
    pl.semaphore_wait(barrier, len(peers_z) + len(peers_p))

    def op_copy(src, dst, send, grp_to):
        copy = pltpu.make_async_remote_copy(
            src_ref=opb.at[src], dst_ref=opb.at[dst], send_sem=send, recv_sem=rx.at[dst],
            device_id={"grp": grp_to, "sub": sub}, device_id_type=MESH,
        )
        copy.start()
        sends.append(copy)

    sends = []

    def go_up(e, c):
        op_copy((e, 0, c), ((e - 1) % NZ, 0, c), tx_up.at[(-e) % NZ, c], in_grp(1, 0))

    def go_down(e, c):
        op_copy((e, 0, c), (e + 1, 0, c), tx_dn.at[e, c], in_grp(NZ - 1, 0))

    def go_sib(e, c):
        op_copy((e, 0, c), (e, 1, c), tx_sib.at[e, c], in_grp(0, 1))

    def got(e, q, c):
        pltpu.make_async_copy(opb.at[e, q, c], opb.at[e, q, c], rx.at[e, q, c]).wait()

    for c in range(CH):
        go_up(0, c)
        go_down(0, c)
        go_sib(0, c)
    for e, q in peers_z:
        pltpu.make_async_remote_copy(
            src_ref=pb.at[in_grp(e, q)], dst_ref=bb.at[(NZ - e) % NZ * 2 + q], send_sem=b_tx, recv_sem=b_rx,
            device_id={"grp": in_grp(e, q), "sub": sub}, device_id_type=MESH,
        ).start()
    bb[0] = pb[grp]

    lane = lax.broadcasted_iota(I32, (16, 256), 1)
    row = lax.broadcasted_iota(I32, (16, 256), 0)
    own_slot = (((((row >> 1) + z) & 7) << 1) | (((row & 1) + core) & 1)) * 16 + sub
    om = jnp.broadcast_to(om_ref[...].astype(F32), (16, 256))
    lane_f = lane.astype(F32)
    own_site = jnp.sum(jnp.where(lane == own_slot, om, 0.0), axis=1, keepdims=True)
    pick = jnp.where(lane_f == own_site, 1.0, 0.0).astype(BF16)
    near = jnp.dot(pick, nt_ref[...].astype(F32).astype(BF16), preferred_element_type=F32)
    for k in range(8):
        slot = jnp.sum(jnp.where(om == near[:, k : k + 1], lane_f, 0.0), axis=1, keepdims=True).astype(I32)
        g_to, s_to = slot >> 4, slot & 15
        rel = ((((g_to >> 1) - z) & 7) << 1) | (((g_to & 1) - core) & 1)
        rel_s = ((((s_to >> 2) - x) & 3) << 2) | (((s_to & 3) - y) & 3)
        hot[16 * k : 16 * k + 16, :] = jnp.where(lane == rel_s * 16 + rel, 1.0, 0.0).astype(BF16)

    def convert(e, q):
        g, at = e // 2, (e % 2) * 128 + q * 64
        for c in range(CH):
            rows = slice(at + 16 * c, at + 16 * c + 16)
            for m in range(5):
                if m < 4:
                    piece = opb[e, q, c, 16 * m : 16 * m + 16, :]
                else:
                    tail = opb[e, q, c, 64:72, :]
                    piece = jnp.concatenate([tail, pltpu.roll(tail, 64, 1)], axis=0)
                high, low = split(piece)
                wh[g, rows, 128 * m : 128 * m + 128] = high
                wl[g, rows, 128 * m : 128 * m + 128] = low

    def take(e, q):
        if q == 1:
            for c in range(CH):
                got(e, 1, c)
        convert(e, q)

    def relay(step):
        for c in range(CH):
            e = NZ - step
            got(e, 0, c)
            if step < 3 or c < CH // 2:
                go_up(e, c)
            go_sib(e, c)
            e = step
            got(e, 0, c)
            if step < 3 or c >= CH // 2:
                go_down(e, c)
            go_sib(e, c)

    def spread(buf, n):
        for dx, dy in peers_p:
            pltpu.make_async_remote_copy(
                src_ref=buf.at[pl.ds(0, 16)], dst_ref=buf.at[pl.ds(((-dx) % NX * NY + (-dy) % NY) * 16, 16)],
                send_sem=z_tx.at[n], recv_sem=z_rx.at[n], device_id=plane(dx, dy), device_id_type=MESH,
            ).start()

    def arrived(buf, n):
        pltpu.make_async_copy(buf.at[pl.ds(16, 240)], buf.at[pl.ds(16, 240)], z_rx.at[n]).wait()

    left128 = lax.broadcasted_iota(I32, (16, 128), 1) < 64

    def segments(value):
        left = lax.broadcasted_iota(I32, (value.shape[0], 128), 1) < 64
        parts = []
        for t in range(value.shape[1] // 128):
            tile = value[:, 128 * t : 128 * t + 128]
            low = jnp.sum(jnp.where(left, tile, 0.0), axis=1, keepdims=True)
            high = jnp.sum(jnp.where(left, 0.0, tile), axis=1, keepdims=True)
            parts.append(jnp.where(left, low, high))
        return parts[0] if len(parts) == 1 else jnp.concatenate(parts, axis=1)

    def total(sums):
        return [segments(jnp.sum(part, axis=0, keepdims=True)) for part in sums]

    def build_x():
        near_h = jnp.dot(hot[...], dh[...], preferred_element_type=F32)
        near_l = jnp.dot(hot[...], dl[...], preferred_element_type=F32)
        for hl, (own, near_v) in enumerate(((dh, near_h), (dl, near_l))):
            for p in range(2):
                cols = slice(128 * p, 128 * p + 128)
                nat = [own[0:16, cols].astype(F32)] + [near_v[16 * k : 16 * k + 16, cols] for k in range(8)]
                rot = [pltpu.roll(part, 64, 1) for part in nat]
                for h in range(2):
                    first, second = (nat, rot) if h == 0 else (rot, nat)
                    at = (hl * 4 + p * 2 + h) * 16
                    for m in range(5):
                        right = second[2 * m + 1] if m < 4 else jnp.zeros((16, 128), F32)
                        xp[at : at + 16, 128 * m : 128 * m + 128] = jnp.where(left128, first[2 * m], right).astype(BF16)

    def apply_group(g, first):
        one = dot_nt(xp[...], wh[g])
        two = dot_nt(xp[0:64, :], wl[g])
        both = one[0:64] + one[64:128] + two
        r = lax.broadcasted_iota(I32, (64, 256), 0) & 15
        c = lax.broadcasted_iota(I32, (64, 256), 1) >> 6
        both = jnp.where(r == c + 4 * g, both, 0.0)
        acc[...] = both if first else acc[...] + both

    def image():
        half = acc[:, 0:128] + acc[:, 128:256]
        half = half + pltpu.roll(half, 64, 1)
        return jnp.concatenate([jnp.where(left128, half[32 * p : 32 * p + 16], half[32 * p + 16 : 32 * p + 32]) for p in range(2)], axis=1)

    rows_of = [slice(32 * i, 32 * i + 32) for i in range(8)]

    take(0, 0)
    take(0, 1)
    relay(1)
    pltpu.make_async_copy(bb.at[pl.ds(1, 15)], bb.at[pl.ds(1, 15)], b_rx).wait()
    for p in range(2):
        z0[0:16, 128 * p : 128 * p + 128] = bb[:, p, :]
    spread(z0, 0)
    for e in (1, 7):
        take(e, 0)
        take(e, 1)
    relay(2)
    for e in (2, 6):
        take(e, 0)
        take(e, 1)
    arrived(z0, 0)
    sums = jnp.zeros((8, 256), F32)
    for rows in rows_of:
        part = z0[rows, :]
        dh[rows, :], dl[rows, :] = split(part)
        sums = sums + fold8(part * part)
    beta = jnp.sqrt(total([sums])[0])
    s0 = 1.0 / beta
    build_x()
    relay(3)
    for e in (3, 5):
        take(e, 0)
        take(e, 1)
    apply_group(0, True)
    apply_group(3, False)
    apply_group(1, False)
    for c in range(CH):
        got(4, 0, c)
        go_sib(4, c)
    take(4, 0)
    take(4, 1)
    apply_group(2, False)

    def apply_all():
        for g in range(4):
            apply_group(g, g == 0)
        return image()

    z1[0:16, :] = image() * s0
    spread(z1, 1)
    arrived(z1, 1)
    sums = jnp.zeros((8, 256), F32)
    for rows in rows_of:
        sums = sums + fold8(z0[rows, :] * z1[rows, :])
    h00 = total([sums])[0] * s0
    f0 = h00 * s0
    sums = jnp.zeros((8, 256), F32)
    for rows in rows_of:
        part = z1[rows, :] - f0 * z0[rows, :]
        w1[rows, :] = part
        dh[rows, :], dl[rows, :] = split(part)
        sums = sums + fold8(part * part)
    build_x()
    h10 = jnp.sqrt(total([sums])[0])
    s1 = 1.0 / h10

    z2[0:16, :] = apply_all() * s1
    spread(z2, 2)
    r0 = jnp.sqrt(h00 * h00 + h10 * h10)
    i0 = 1.0 / r0
    c0, n0 = h00 * i0, h10 * i0
    g0, g1 = c0 * beta, -n0 * beta
    arrived(z2, 2)
    sums0, sums1 = jnp.zeros((8, 256), F32), jnp.zeros((8, 256), F32)
    for rows in rows_of:
        part = z2[rows, :]
        sums0 = sums0 + fold8(z0[rows, :] * part)
        sums1 = sums1 + fold8(w1[rows, :] * part)
    h01, h11 = total([sums0, sums1])
    h01, h11 = h01 * s0, h11 * s1
    f0, f1 = h01 * s0, h11 * s1
    sums = jnp.zeros((8, 256), F32)
    for rows in rows_of:
        part = z2[rows, :] - f0 * z0[rows, :] - f1 * w1[rows, :]
        if rows.start == 0:
            w2[...] = part[0:16]
        dh[rows, :], dl[rows, :] = split(part)
        sums = sums + fold8(part * part)
    build_x()
    h21 = jnp.sqrt(total([sums])[0])
    s2 = 1.0 / h21

    last = apply_all() * s2
    basis = [z0[0:16, :] * s0, w1[0:16, :] * s1, w2[...] * s2]
    sums = [jnp.sum(fold8(part * last), axis=0, keepdims=True) for part in basis + [last]]
    pd[0] = jnp.concatenate([part[:, 128 * p : 128 * p + 128] for part in sums for p in range(2)], axis=0)
    for dx, dy in peers_p:
        pltpu.make_async_remote_copy(
            src_ref=pd.at[0], dst_ref=pd.at[(-dx) % NX * NY + (-dy) % NY],
            send_sem=z_tx.at[3], recv_sem=z_rx.at[3], device_id=plane(dx, dy), device_id_type=MESH,
        ).start()
    t0, t1 = c0 * h01 + n0 * h11, c0 * h11 - n0 * h01
    r1 = jnp.sqrt(t1 * t1 + h21 * h21)
    i1 = 1.0 / r1
    c1, n1 = t1 * i1, h21 * i1
    g1, g2 = c1 * g1, -n1 * g1
    pltpu.make_async_copy(pd.at[pl.ds(1, 15)], pd.at[pl.ds(1, 15)], z_rx.at[3]).wait()
    dots = segments(jnp.sum(pd[...], axis=0))
    h02, h12, h22, zz = [jnp.concatenate([dots[2 * i : 2 * i + 1], dots[2 * i + 1 : 2 * i + 2]], axis=1) for i in range(4)]
    norm_sq = jnp.maximum(zz - h02 * h02 - h12 * h12 - h22 * h22, 0.0)
    u0, u1 = c0 * h02 + n0 * h12, c0 * h12 - n0 * h02
    u1, u2 = c1 * u1 + n1 * h22, c1 * h22 - n1 * u1
    y2 = u2 * g2 / (u2 * u2 + norm_sq)
    y1 = (g1 - u1 * y2) * i1
    y0 = (g0 - t0 * y1 - u0 * y2) * i0
    result = y0 * basis[0] + y1 * basis[1] + y2 * basis[2]
    for p in range(2):
        sb[:, p, :] = result[:, 128 * p : 128 * p + 128]
    for e, q in peers_z:
        pltpu.make_async_remote_copy(
            src_ref=sb.at[2 * e + q], dst_ref=ob.at[grp], send_sem=s_tx, recv_sem=s_rx,
            device_id={"grp": in_grp(e, q), "sub": sub}, device_id_type=MESH,
        ).start()
    ob[grp] = sb[0]
    for copy in sends:
        copy.wait_send()
    pltpu.make_async_copy(pb.at[pl.ds(1, 15)], pb.at[pl.ds(1, 15)], b_tx).wait()
    for n, buf in enumerate((z0, z1, z2)):
        pltpu.make_async_copy(buf.at[pl.ds(16, 240)], buf.at[pl.ds(16, 240)], z_tx.at[n]).wait()
    pltpu.make_async_copy(pd.at[pl.ds(1, 15)], pd.at[pl.ds(1, 15)], z_tx.at[3]).wait()
    pltpu.make_async_copy(sb.at[pl.ds(1, 15)], sb.at[pl.ds(1, 15)], s_tx).wait()
    pltpu.make_async_copy(ob.at[pl.ds(1, 15)], ob.at[pl.ds(1, 15)], s_rx).wait()
    tiles = [ob[:, p, :] for p in range(2)]
    out_ref[0] = jnp.concatenate(
        [tiles[0][:, 0:64], tiles[0][:, 64:128], tiles[1][:, 0:64], tiles[1][:, 64:128]], axis=0
    ).T


def per_device(coarse_op, right_side, owner_map, neighbor_table):
    vmem = pl.BlockSpec(memory_space=pltpu.VMEM)
    dma = pltpu.SemaphoreType.DMA
    return pl.pallas_call(
        kernel,
        out_shape=jax.ShapeDtypeStruct((1, 64, 64), F32),
        in_specs=[pl.BlockSpec(memory_space=pl.ANY), vmem, vmem, vmem],
        out_specs=vmem,
        scratch_shapes=[
            pltpu.VMEM((64, 576), F32),
            pltpu.VMEM((NZ, 2, CH, 72, 128), F32),
            pltpu.VMEM((4, 256, 640), BF16),
            pltpu.VMEM((4, 256, 640), BF16),
            pltpu.VMEM((16, 2, 128), F32),
            pltpu.VMEM((16, 2, 128), F32),
            pltpu.VMEM((256, 256), F32),
            pltpu.VMEM((256, 256), F32),
            pltpu.VMEM((256, 256), F32),
            pltpu.VMEM((256, 256), F32),
            pltpu.VMEM((16, 256), F32),
            pltpu.VMEM((256, 256), BF16),
            pltpu.VMEM((256, 256), BF16),
            pltpu.VMEM((128, 256), BF16),
            pltpu.VMEM((128, 640), BF16),
            pltpu.VMEM((64, 256), F32),
            pltpu.VMEM((16, 8, 128), F32),
            pltpu.VMEM((16, 2, 128), F32),
            pltpu.VMEM((16, 2, 128), F32),
            dma((NZ, 2, CH)),
            dma((4, CH)),
            dma((4, CH)),
            dma((NZ, CH)),
            dma,
            dma,
            dma,
            dma((4,)),
            dma((4,)),
            dma,
            dma,
        ],
        compiler_params=pltpu.CompilerParams(collective_id=0, has_side_effects=True),
    )(coarse_op, right_side, owner_map.reshape(1, 256), neighbor_table)


def solution(mesh):
    placed = (P(("grp", "sub"), None, None), P(("grp", "sub"), None, None), P(), P())
    return jax.shard_map(
        per_device,
        mesh=mesh,
        in_specs=placed,
        out_specs=P(("grp", "sub"), None, None),
        check_vma=False,
    )
```

time: 242 us -> 62 us (0.26)
  waiting for transfers between devices: 71.7 us -> 0 us
  Pallas kernels: 0 us -> 58.9 us
  starting transfers between devices: 58.7 us -> 0 us
  blocking collectives: 35.2 us -> 0 us
  local copies, waits for them, and re-layouts: 34.1 us -> 2.84 us
  other arithmetic: 15.4 us -> 0 us
  between operations: 14 us -> 0.01 us
  matrix products: 11.5 us -> 0 us
    all_to_all x13 -> x0, waiting for transfers between devices: 71 us -> none  [the longest x12 66.9 us: from_everyone(): return lax.all_to_all(copies, axis, split_axis=0, concat_axis=0, tiled=True)]
    pallas_call x0 -> x1, Pallas kernels: none -> 58.9 us  [per_device(): pl.pallas_call(kernel, out_shape=jax.ShapeDtypeStruct((1, 64, 64), F32),...]
    all_to_all x13 -> x0, starting transfers between devices: 58.7 us -> none  [the longest x12 48.7 us: from_everyone(): return lax.all_to_all(copies, axis, split_axis=0, concat_axis=0, tiled=True)]
    all_to_all x2 -> x0, blocking collectives: 35.2 us -> none  [the longest x1 25.4 us: per_device(): lax.all_to_all(solution, 'grp', split_axis=0, concat_axis=2, tiled=True)]
    gather x4 -> x0, local copies, waits for them, and re-layouts: 14.5 us -> none  [the longest x3 14 us: per_device(): link = inverse[neighbor_table[owner_map]]]
    dot_general x7 -> x0, matrix products: 11.3 us -> none  [the longest x3 10.1 us: per_device(): jnp.einsum('sac,scr->sar', op_rows, stacked, precision=lax.Precision.HIGH...]
    broadcast_in_dim x10 -> x0, local copies, waits for them, and re-layouts: 5.46 us -> none  [from_everyone(): copies = jnp.broadcast_to(array, (lax.axis_size(axis), *array.shape))]
    all_to_all x5 -> x0, other arithmetic: 5.28 us -> none  [the longest x3 3.86 us: from_everyone(): return lax.all_to_all(copies, axis, split_axis=0, concat_axis=0, tiled=True)]
  transfers between devices with their start and end apart: 14 -> 0, of which waited for: 12 -> 0; matrix products, arithmetic and copies ran while one was open for 13% -> 0% of each run, Pallas kernels for 0% -> 0%
where the time goes in v1:
time: 62 us; the launch traced here: 61.8 us
  Pallas kernels  58.9 us (95%)
  local copies, waits for them, and re-layouts  2.84 us (5%)
    pallas_call x1, Pallas kernels, per_device(): pl.pallas_call(kernel, out_shape=jax.ShapeDtypeStruct((1, 64, 64), F32),...  58.9 us
    unnamed x2, local copies, waits for them, and re-layouts  2.84 us

profile of v1, /device:TPU:1, one launch (start us, length us, event | category | flops | bytes accessed | tf_op | source)
XLA Modules:
  0.0 61.8 jit_solution(15108864822123396028)
XLA Ops:
  0.0 1.5 %copy.5.nt_ref = s32[256,8]{1,0:T(8,128)} copy(s32[256,8]{0,1:T(8,128)} %param.7) | data formatting | bytes 16384 | tf_op args[3]
  1.5 58.9 %shard_map.46 = f32[1,64,64]{2,1,0:T(8,128)} custom-call(f32[1,64,576]{2,1,0:T(8,128)} %op_hbm.1, f32[1,64,64]{2,1,0:T(8,128)} %b_ref.1, s32[1,256]{1,0:T(1,128)} %bitcast.1, s32[256,8]{1,0:T(8,128)} %copy.5.nt_ref), custom_call_target="tpu_custom_call" | custom-call | tf_op jit(solution)/shard_map/pallas_call | solution.py:337
  60.4 1.4 %copy.7 = f32[1,64,64]{2,1,0:T(8,128)} copy(f32[1,64,64]{2,1,0:T(8,128)} %shard_map.46) | data formatting | bytes 32768

commit v2 on v1

--- a/solution.py
+++ b/solution.py
@@ -25,8 +25,8 @@
 
 
 def kernel(
-    op_hbm, b_ref, om_ref, nt_ref, out_ref,
-    opv, opb, wh, wl, pb, bb, z0, z1, z2, w1, w2, dh, dl, hot, xp, acc, pd, sb, ob,
+    op_hbm, b_hbm, om_hbm, nt_hbm, out_ref,
+    b_ref, om_ref, nt_ref, opv, opb, wh, wl, pb, bb, z0, z1, z2, w1, w2, dh, dl, hot, xp, acc, pd, sb, ob,
     rx, tx_up, tx_dn, tx_sib, ld_sem, b_tx, b_rx, z_tx, z_rx, s_tx, s_rx,
 ):
     grp, sub = lax.axis_index("grp"), lax.axis_index("sub")
@@ -36,24 +36,33 @@
     def in_grp(e, q):
         return (z + e) % NZ * 2 + (core + q) % 2
 
+    def hops(*steps):
+        return sum(min(step, size - step) for step, size in steps)
+
     peers_z = [(e, q) for e in range(NZ) for q in range(2) if (e, q) != (0, 0)]
     peers_p = [(dx, dy) for dx in range(NX) for dy in range(NY) if (dx, dy) != (0, 0)]
+    peers_z.sort(key=lambda peer: -hops((peer[0], NZ)))
+    peers_p.sort(key=lambda peer: -hops((peer[0], NX), (peer[1], NY)))
 
     def plane(dx, dy):
         return {"grp": grp, "sub": (x + dx) % NX * NY + (y + dy) % NY}
 
-    load = pltpu.make_async_copy(op_hbm.at[0], opv, ld_sem)
-    load.start()
     barrier = pltpu.get_barrier_semaphore()
     for e, q in peers_z:
         pl.semaphore_signal(barrier, inc=1, device_id={"grp": in_grp(e, q), "sub": sub}, device_id_type=MESH)
     for dx, dy in peers_p:
         pl.semaphore_signal(barrier, inc=1, device_id=plane(dx, dy), device_id_type=MESH)
 
-    bt = b_ref[0].T
+    ins = ((b_hbm.at[0], b_ref), (op_hbm.at[0], opv), (om_hbm, om_ref), (nt_hbm, nt_ref))
+    loads = [pltpu.make_async_copy(src, dst, ld_sem.at[n]) for n, (src, dst) in enumerate(ins)]
+    for load in loads:
+        load.start()
+
+    loads[0].wait()
+    bt = b_ref[...].T
     for p in range(2):
         pb[:, p, :] = jnp.concatenate([bt[32 * p : 32 * p + 16], bt[32 * p + 16 : 32 * p + 32]], axis=1)
-    load.wait()
+    loads[1].wait()
     for c in range(CH):
         for m in range(4):
             opb[0, 0, c, 16 * m : 16 * m + 16, :] = opv[16 * c : 16 * c + 16, 128 * m : 128 * m + 128]
@@ -84,17 +93,19 @@
     def got(e, q, c):
         pltpu.make_async_copy(opb.at[e, q, c], opb.at[e, q, c], rx.at[e, q, c]).wait()
 
-    for c in range(CH):
-        go_up(0, c)
-        go_down(0, c)
-        go_sib(0, c)
     for e, q in peers_z:
         pltpu.make_async_remote_copy(
             src_ref=pb.at[in_grp(e, q)], dst_ref=bb.at[(NZ - e) % NZ * 2 + q], send_sem=b_tx, recv_sem=b_rx,
             device_id={"grp": in_grp(e, q), "sub": sub}, device_id_type=MESH,
         ).start()
+    for c in range(CH):
+        go_up(0, c)
+        go_down(0, c)
+        go_sib(0, c)
     bb[0] = pb[grp]
 
+    loads[2].wait()
+    loads[3].wait()
     lane = lax.broadcasted_iota(I32, (16, 256), 1)
     row = lax.broadcasted_iota(I32, (16, 256), 0)
     own_slot = (((((row >> 1) + z) & 7) << 1) | (((row & 1) + core) & 1)) * 16 + sub
@@ -102,7 +113,7 @@
     lane_f = lane.astype(F32)
     own_site = jnp.sum(jnp.where(lane == own_slot, om, 0.0), axis=1, keepdims=True)
     pick = jnp.where(lane_f == own_site, 1.0, 0.0).astype(BF16)
-    near = jnp.dot(pick, nt_ref[...].astype(F32).astype(BF16), preferred_element_type=F32)
+    near = dot_nt(pick, nt_ref[...].astype(F32).astype(BF16))
     for k in range(8):
         slot = jnp.sum(jnp.where(om == near[:, k : k + 1], lane_f, 0.0), axis=1, keepdims=True).astype(I32)
         g_to, s_to = slot >> 4, slot & 15
@@ -110,25 +121,24 @@
         rel_s = ((((s_to >> 2) - x) & 3) << 2) | (((s_to & 3) - y) & 3)
         hot[16 * k : 16 * k + 16, :] = jnp.where(lane == rel_s * 16 + rel, 1.0, 0.0).astype(BF16)
 
-    def convert(e, q):
-        g, at = e // 2, (e % 2) * 128 + q * 64
+    def take(e):
         for c in range(CH):
-            rows = slice(at + 16 * c, at + 16 * c + 16)
-            for m in range(5):
-                if m < 4:
-                    piece = opb[e, q, c, 16 * m : 16 * m + 16, :]
-                else:
-                    tail = opb[e, q, c, 64:72, :]
-                    piece = jnp.concatenate([tail, pltpu.roll(tail, 64, 1)], axis=0)
-                high, low = split(piece)
-                wh[g, rows, 128 * m : 128 * m + 128] = high
-                wl[g, rows, 128 * m : 128 * m + 128] = low
-
-    def take(e, q):
-        if q == 1:
-            for c in range(CH):
-                got(e, 1, c)
-        convert(e, q)
+            got(e, 1, c)
+        at = slice(e % 2 * 128, e % 2 * 128 + 128)
+        for m in range(5):
+            pieces = []
+            for q in range(2):
+                for c in range(CH):
+                    if m < 4:
+                        pieces.append(opb[e, q, c, 16 * m : 16 * m + 16, :])
+                    else:
+                        tail = opb[e, q, c, 64:72, :]
+                        pieces += [tail, pltpu.roll(tail, 64, 1)]
+            turned = jnp.concatenate(pieces, axis=0).T
+            depth = 128 if m < 4 else 64
+            high, low = split(turned[0:depth])
+            wh[e // 2, 128 * m : 128 * m + depth, at] = high
+            wl[e // 2, 128 * m : 128 * m + depth, at] = low
 
     def relay(step):
         for c in range(CH):
@@ -179,13 +189,14 @@
                 for h in range(2):
                     first, second = (nat, rot) if h == 0 else (rot, nat)
                     at = (hl * 4 + p * 2 + h) * 16
-                    for m in range(5):
-                        right = second[2 * m + 1] if m < 4 else jnp.zeros((16, 128), F32)
-                        xp[at : at + 16, 128 * m : 128 * m + 128] = jnp.where(left128, first[2 * m], right).astype(BF16)
+                    for m in range(4):
+                        both = jnp.where(left128, first[2 * m], second[2 * m + 1])
+                        xp[at : at + 16, 128 * m : 128 * m + 128] = both.astype(BF16)
+                    xp[at : at + 16, 512:576] = first[8][:, 0:64].astype(BF16)
 
     def apply_group(g, first):
-        one = dot_nt(xp[...], wh[g])
-        two = dot_nt(xp[0:64, :], wl[g])
+        one = jnp.dot(xp[...], wh[g], preferred_element_type=F32)
+        two = jnp.dot(xp[0:64, :], wl[g], preferred_element_type=F32)
         both = one[0:64] + one[64:128] + two
         r = lax.broadcasted_iota(I32, (64, 256), 0) & 15
         c = lax.broadcasted_iota(I32, (64, 256), 1) >> 6
@@ -199,20 +210,17 @@
 
     rows_of = [slice(32 * i, 32 * i + 32) for i in range(8)]
 
-    take(0, 0)
-    take(0, 1)
+    take(0)
     relay(1)
     pltpu.make_async_copy(bb.at[pl.ds(1, 15)], bb.at[pl.ds(1, 15)], b_rx).wait()
     for p in range(2):
         z0[0:16, 128 * p : 128 * p + 128] = bb[:, p, :]
     spread(z0, 0)
     for e in (1, 7):
-        take(e, 0)
-        take(e, 1)
+        take(e)
     relay(2)
     for e in (2, 6):
-        take(e, 0)
-        take(e, 1)
+        take(e)
     arrived(z0, 0)
     sums = jnp.zeros((8, 256), F32)
     for rows in rows_of:
@@ -224,16 +232,14 @@
     build_x()
     relay(3)
     for e in (3, 5):
-        take(e, 0)
-        take(e, 1)
+        take(e)
     apply_group(0, True)
     apply_group(3, False)
     apply_group(1, False)
     for c in range(CH):
         got(4, 0, c)
         go_sib(4, c)
-    take(4, 0)
-    take(4, 1)
+    take(4)
     apply_group(2, False)
 
     def apply_all():
@@ -337,13 +343,16 @@
     return pl.pallas_call(
         kernel,
         out_shape=jax.ShapeDtypeStruct((1, 64, 64), F32),
-        in_specs=[pl.BlockSpec(memory_space=pl.ANY), vmem, vmem, vmem],
+        in_specs=[pl.BlockSpec(memory_space=pl.ANY)] * 4,
         out_specs=vmem,
         scratch_shapes=[
+            pltpu.VMEM((64, 64), F32),
+            pltpu.VMEM((1, 256), I32),
+            pltpu.VMEM((8, 256), I32),
             pltpu.VMEM((64, 576), F32),
             pltpu.VMEM((NZ, 2, CH, 72, 128), F32),
-            pltpu.VMEM((4, 256, 640), BF16),
-            pltpu.VMEM((4, 256, 640), BF16),
+            pltpu.VMEM((4, 576, 256), BF16),
+            pltpu.VMEM((4, 576, 256), BF16),
             pltpu.VMEM((16, 2, 128), F32),
             pltpu.VMEM((16, 2, 128), F32),
             pltpu.VMEM((256, 256), F32),
@@ -354,7 +363,7 @@
             pltpu.VMEM((256, 256), BF16),
             pltpu.VMEM((256, 256), BF16),
             pltpu.VMEM((128, 256), BF16),
-            pltpu.VMEM((128, 640), BF16),
+            pltpu.VMEM((128, 576), BF16),
             pltpu.VMEM((64, 256), F32),
             pltpu.VMEM((16, 8, 128), F32),
             pltpu.VMEM((16, 2, 128), F32),
@@ -363,7 +372,7 @@
             dma((4, CH)),
             dma((4, CH)),
             dma((NZ, CH)),
-            dma,
+            dma((4,)),
             dma,
             dma,
             dma((4,)),
@@ -372,7 +381,7 @@
             dma,
         ],
         compiler_params=pltpu.CompilerParams(collective_id=0, has_side_effects=True),
-    )(coarse_op, right_side, owner_map.reshape(1, 256), neighbor_table)
+    )(coarse_op, right_side, owner_map.reshape(1, 256), neighbor_table.T)
 
 
 def solution(mesh):

time: 62 us -> 55.1 us (0.89)
  Pallas kernels: 58.9 us -> 53.6 us
  local copies, waits for them, and re-layouts: 2.84 us -> 1.38 us
    pallas_call x1, Pallas kernels: 58.9 us -> 53.6 us  [per_device(): pl.pallas_call(kernel, out_shape=jax.ShapeDtypeStruct((1, 64, 64), F32),...]
    unnamed x2 -> x1, local copies, waits for them, and re-layouts: 2.84 us -> 1.38 us
where the time goes in v2:
time: 55.1 us; the launch traced here: 54.9 us
  Pallas kernels  53.6 us (97%)
  local copies, waits for them, and re-layouts  1.38 us (3%)
    pallas_call x1, Pallas kernels, per_device(): pl.pallas_call(kernel, out_shape=jax.ShapeDtypeStruct((1, 64, 64), F32),...  53.6 us
    unnamed x1, local copies, waits for them, and re-layouts  1.38 us

profile of v2, /device:TPU:1, one launch (start us, length us, event | category | flops | bytes accessed | tf_op | source)
XLA Modules:
  0.0 54.9 jit_solution(2031041721497603721)
XLA Ops:
  0.0 53.6 %shard_map.46 = f32[1,64,64]{2,1,0:T(8,128)} custom-call(f32[1,64,576]{2,1,0:T(8,128)} %op_hbm.1, f32[1,64,64]{2,1,0:T(8,128)} %b_hbm.1, s32[1,256]{1,0:T(1,128)} %bitcast.3, s32[8,256]{1,0:T(8,128)} %bitcast.2), custom_call_target="tpu_custom_call" | custom-call | tf_op jit(solution)/shard_map/pallas_call | solution.py:343
  53.6 1.4 %copy.6 = f32[1,64,64]{2,1,0:T(8,128)} copy(f32[1,64,64]{2,1,0:T(8,128)} %shard_map.46) | data formatting | bytes 32768

commit v3 on v2

--- a/solution.py
+++ b/solution.py
@@ -7,7 +7,7 @@
 
 MESH = pl.DeviceIdType.MESH
 NZ, NX, NY = 8, 4, 4
-CH = 4
+CH = 9
 F32, BF16, I32 = jnp.float32, jnp.bfloat16, jnp.int32
 
 
@@ -27,7 +27,7 @@
 def kernel(
     op_hbm, b_hbm, om_hbm, nt_hbm, out_ref,
     b_ref, om_ref, nt_ref, opv, opb, wh, wl, pb, bb, z0, z1, z2, w1, w2, dh, dl, hot, xp, acc, pd, sb, ob,
-    rx, tx_up, tx_dn, tx_sib, ld_sem, b_tx, b_rx, z_tx, z_rx, s_tx, s_rx,
+    rx, rx4, sib_rx, op_tx, ld_sem, b_tx, b_rx, z_tx, z_rx, s_tx, s_rx,
 ):
     grp, sub = lax.axis_index("grp"), lax.axis_index("sub")
     z, core = grp // 2, grp % 2
@@ -63,45 +63,52 @@
     for p in range(2):
         pb[:, p, :] = jnp.concatenate([bt[32 * p : 32 * p + 16], bt[32 * p + 16 : 32 * p + 32]], axis=1)
     loads[1].wait()
-    for c in range(CH):
-        for m in range(4):
-            opb[0, 0, c, 16 * m : 16 * m + 16, :] = opv[16 * c : 16 * c + 16, 128 * m : 128 * m + 128]
-        opb[0, 0, c, 64:72, :] = jnp.concatenate(
-            [opv[16 * c : 16 * c + 8, 512:576], opv[16 * c + 8 : 16 * c + 16, 512:576]], axis=1
-        )
+    for c in range(CH - 1):
+        rows, m = c % 2 * 32, c // 2 * 128
+        opb[0, 0, c] = opv[rows : rows + 32, m : m + 128]
+    opb[0, 0, CH - 1] = jnp.concatenate([opv[0:32, 512:576], opv[32:64, 512:576]], axis=1)
     pl.semaphore_wait(barrier, len(peers_z) + len(peers_p))
 
-    def op_copy(src, dst, send, grp_to):
-        copy = pltpu.make_async_remote_copy(
-            src_ref=opb.at[src], dst_ref=opb.at[dst], send_sem=send, recv_sem=rx.at[dst],
+    sent = []
+
+    def op_copy(e, to, q, c, count, sem, grp_to):
+        pltpu.make_async_remote_copy(
+            src_ref=opb.at[e, 0, pl.ds(c, count)], dst_ref=opb.at[to, q, pl.ds(c, count)], send_sem=op_tx, recv_sem=sem,
             device_id={"grp": grp_to, "sub": sub}, device_id_type=MESH,
-        )
-        copy.start()
-        sends.append(copy)
-
-    sends = []
-
-    def go_up(e, c):
-        op_copy((e, 0, c), ((e - 1) % NZ, 0, c), tx_up.at[(-e) % NZ, c], in_grp(1, 0))
-
-    def go_down(e, c):
-        op_copy((e, 0, c), (e + 1, 0, c), tx_dn.at[e, c], in_grp(NZ - 1, 0))
-
-    def go_sib(e, c):
-        op_copy((e, 0, c), (e, 1, c), tx_sib.at[e, c], in_grp(0, 1))
-
-    def got(e, q, c):
-        pltpu.make_async_copy(opb.at[e, q, c], opb.at[e, q, c], rx.at[e, q, c]).wait()
+        ).start()
+        sent.append(count)
+
+    def ring(e, to, c, count, grp_to):
+        if to == 4:
+            for at in range(c, c + count):
+                if (at < CH // 2) == (e == 5):
+                    op_copy(e, to, 0, at, 1, rx4.at[at], grp_to)
+        else:
+            op_copy(e, to, 0, c, count, rx.at[to, c // 2], grp_to)
+
+    def go_up(e, c, count):
+        ring(e, (e - 1) % NZ, c, count, in_grp(1, 0))
+
+    def go_down(e, c, count):
+        ring(e, e + 1, c, count, in_grp(NZ - 1, 0))
+
+    def go_sib(e, c, count):
+        op_copy(e, e, 1, c, count, sib_rx.at[e], in_grp(0, 1))
+
+    def got(ref, sem):
+        pltpu.make_async_copy(ref, ref, sem).wait()
+
+    pieces_of = [(c, min(2, CH - c)) for c in range(0, CH, 2)]
 
     for e, q in peers_z:
         pltpu.make_async_remote_copy(
             src_ref=pb.at[in_grp(e, q)], dst_ref=bb.at[(NZ - e) % NZ * 2 + q], send_sem=b_tx, recv_sem=b_rx,
             device_id={"grp": in_grp(e, q), "sub": sub}, device_id_type=MESH,
         ).start()
-    for c in range(CH):
-        go_up(0, c)
-        go_down(0, c)
-        go_sib(0, c)
+    for c, count in pieces_of:
+        go_up(0, c, count)
+        go_down(0, c, count)
+        go_sib(0, c, count)
     bb[0] = pb[grp]
 
     loads[2].wait()
@@ -122,18 +129,15 @@
         hot[16 * k : 16 * k + 16, :] = jnp.where(lane == rel_s * 16 + rel, 1.0, 0.0).astype(BF16)
 
     def take(e):
-        for c in range(CH):
-            got(e, 1, c)
         at = slice(e % 2 * 128, e % 2 * 128 + 128)
+        got(opb.at[e, 1], sib_rx.at[e])
         for m in range(5):
             pieces = []
             for q in range(2):
-                for c in range(CH):
-                    if m < 4:
-                        pieces.append(opb[e, q, c, 16 * m : 16 * m + 16, :])
-                    else:
-                        tail = opb[e, q, c, 64:72, :]
-                        pieces += [tail, pltpu.roll(tail, 64, 1)]
+                for c in range(2 * m, min(2 * m + 2, CH)):
+                    pieces.append(opb[e, q, c])
+                    if m == 4:
+                        pieces.append(pltpu.roll(pieces[-1], 64, 1))
             turned = jnp.concatenate(pieces, axis=0).T
             depth = 128 if m < 4 else 64
             high, low = split(turned[0:depth])
@@ -141,29 +145,29 @@
             wl[e // 2, 128 * m : 128 * m + depth, at] = low
 
     def relay(step):
-        for c in range(CH):
-            e = NZ - step
-            got(e, 0, c)
-            if step < 3 or c < CH // 2:
-                go_up(e, c)
-            go_sib(e, c)
-            e = step
-            got(e, 0, c)
-            if step < 3 or c >= CH // 2:
-                go_down(e, c)
-            go_sib(e, c)
-
-    def spread(buf, n):
+        for c, count in pieces_of:
+            for e, go in ((NZ - step, go_up), (step, go_down)):
+                got(opb.at[e, 0, pl.ds(c, count)], rx.at[e, c // 2])
+                go(e, c, count)
+                go_sib(e, c, count)
+
+    def last_block(*pieces):
+        for c in pieces:
+            got(opb.at[4, 0, c], rx4.at[c])
+            go_sib(4, c, 1)
+
+    def spread(buf, n, at=0, count=16):
         for dx, dy in peers_p:
             pltpu.make_async_remote_copy(
-                src_ref=buf.at[pl.ds(0, 16)], dst_ref=buf.at[pl.ds(((-dx) % NX * NY + (-dy) % NY) * 16, 16)],
+                src_ref=buf.at[pl.ds(at, count)],
+                dst_ref=buf.at[pl.ds(((-dx) % NX * NY + (-dy) % NY) * 16 + at, count)],
                 send_sem=z_tx.at[n], recv_sem=z_rx.at[n], device_id=plane(dx, dy), device_id_type=MESH,
             ).start()
 
     def arrived(buf, n):
         pltpu.make_async_copy(buf.at[pl.ds(16, 240)], buf.at[pl.ds(16, 240)], z_rx.at[n]).wait()
 
-    left128 = lax.broadcasted_iota(I32, (16, 128), 1) < 64
+    left8 = lax.broadcasted_iota(I32, (8, 128), 1) < 64
 
     def segments(value):
         left = lax.broadcasted_iota(I32, (value.shape[0], 128), 1) < 64
@@ -186,27 +190,36 @@
                 cols = slice(128 * p, 128 * p + 128)
                 nat = [own[0:16, cols].astype(F32)] + [near_v[16 * k : 16 * k + 16, cols] for k in range(8)]
                 rot = [pltpu.roll(part, 64, 1) for part in nat]
-                for h in range(2):
-                    first, second = (nat, rot) if h == 0 else (rot, nat)
-                    at = (hl * 4 + p * 2 + h) * 16
+                for half in range(2):
+                    some = slice(8 * half, 8 * half + 8)
+                    at = slice((hl * 2 + p) * 16, (hl * 2 + p) * 16 + 16)
                     for m in range(4):
-                        both = jnp.where(left128, first[2 * m], second[2 * m + 1])
-                        xp[at : at + 16, 128 * m : 128 * m + 128] = both.astype(BF16)
-                    xp[at : at + 16, 512:576] = first[8][:, 0:64].astype(BF16)
-
-    def apply_group(g, first):
-        one = jnp.dot(xp[...], wh[g], preferred_element_type=F32)
-        two = jnp.dot(xp[0:64, :], wl[g], preferred_element_type=F32)
-        both = one[0:64] + one[64:128] + two
-        r = lax.broadcasted_iota(I32, (64, 256), 0) & 15
-        c = lax.broadcasted_iota(I32, (64, 256), 1) >> 6
-        both = jnp.where(r == c + 4 * g, both, 0.0)
-        acc[...] = both if first else acc[...] + both
-
-    def image():
-        half = acc[:, 0:128] + acc[:, 128:256]
-        half = half + pltpu.roll(half, 64, 1)
-        return jnp.concatenate([jnp.where(left128, half[32 * p : 32 * p + 16], half[32 * p + 16 : 32 * p + 32]) for p in range(2)], axis=1)
+                        a, b = 2 * m, 2 * m + 1
+                        low = jnp.where(left8, nat[a][some], rot[b][some])
+                        high = jnp.where(left8, rot[a][some], nat[b][some])
+                        xp[half, at, 128 * m : 128 * m + 128] = jnp.concatenate([low, high], axis=0).astype(BF16)
+                    both = jnp.concatenate([nat[8][some], rot[8][some]], axis=0)
+                    xp[half, at, 512:576] = both[:, 0:64].astype(BF16)
+
+    def apply_group(g):
+        half = g // 2
+        one = jnp.dot(xp[half], wh[g], preferred_element_type=F32)
+        two = jnp.dot(xp[half, 0:32, :], wl[g], preferred_element_type=F32)
+        both = one[0:32] + one[32:64] + two
+        r = lax.broadcasted_iota(I32, (32, 256), 0) & 7
+        c = lax.broadcasted_iota(I32, (32, 256), 1) >> 6
+        return jnp.where(r == c + 4 * (g % 2), both, 0.0)
+
+    def image(both):
+        both = both[:, 0:128] + both[:, 128:256]
+        both = both + pltpu.roll(both, 64, 1)
+        return jnp.concatenate(
+            [jnp.where(left8, both[16 * p : 16 * p + 8], both[16 * p + 8 : 16 * p + 16]) for p in range(2)], axis=1
+        )
+
+    def apply_all():
+        groups = [apply_group(g) for g in range(4)]
+        return [image(groups[0] + groups[1]), image(groups[2] + groups[3])]
 
     rows_of = [slice(32 * i, 32 * i + 32) for i in range(8)]
 
@@ -216,56 +229,58 @@
     for p in range(2):
         z0[0:16, 128 * p : 128 * p + 128] = bb[:, p, :]
     spread(z0, 0)
-    for e in (1, 7):
-        take(e)
     relay(2)
-    for e in (2, 6):
-        take(e)
+    take(1)
+    take(7)
+    relay(3)
+    take(2)
+    take(6)
     arrived(z0, 0)
     sums = jnp.zeros((8, 256), F32)
     for rows in rows_of:
         part = z0[rows, :]
         dh[rows, :], dl[rows, :] = split(part)
         sums = sums + fold8(part * part)
+    build_x()
     beta = jnp.sqrt(total([sums])[0])
     s0 = 1.0 / beta
-    build_x()
-    relay(3)
-    for e in (3, 5):
-        take(e)
-    apply_group(0, True)
-    apply_group(3, False)
-    apply_group(1, False)
-    for c in range(CH):
-        got(4, 0, c)
-        go_sib(4, c)
+    acc[...] = apply_group(0)
+    last_block(0, 4)
+    take(3)
+    last_block(1, 5)
+    z1[0:8, :] = image(acc[...] + apply_group(1)) * s0
+    spread(z1, 1, 0, 8)
+    last_block(2, 6, 3, 7, 8)
+    take(5)
+    acc[...] = apply_group(3)
     take(4)
-    apply_group(2, False)
-
-    def apply_all():
-        for g in range(4):
-            apply_group(g, g == 0)
-        return image()
-
-    z1[0:16, :] = image() * s0
-    spread(z1, 1)
+
+    z1[8:16, :] = image(acc[...] + apply_group(2)) * s0
+    spread(z1, 1, 8, 8)
+    slots, rest = divmod(sum(sent), 2 * CH)
+    got(opb.at[pl.ds(0, slots)], op_tx)
+    if rest:
+        got(opb.at[0, 0, pl.ds(0, rest)], op_tx)
     arrived(z1, 1)
     sums = jnp.zeros((8, 256), F32)
     for rows in rows_of:
-        sums = sums + fold8(z0[rows, :] * z1[rows, :])
+        part = z1[rows, :]
+        dh[rows, :], dl[rows, :] = split(part)
+        sums = sums + fold8(z0[rows, :] * part)
+    build_x()
     h00 = total([sums])[0] * s0
     f0 = h00 * s0
     sums = jnp.zeros((8, 256), F32)
     for rows in rows_of:
         part = z1[rows, :] - f0 * z0[rows, :]
         w1[rows, :] = part
-        dh[rows, :], dl[rows, :] = split(part)
         sums = sums + fold8(part * part)
-    build_x()
     h10 = jnp.sqrt(total([sums])[0])
     s1 = 1.0 / h10
 
-    z2[0:16, :] = apply_all() * s1
+    for half, part in enumerate(apply_all()):
+        some = slice(8 * half, 8 * half + 8)
+        z2[some, :] = (part - h00 * z1[some, :]) * s1
     spread(z2, 2)
     r0 = jnp.sqrt(h00 * h00 + h10 * h10)
     i0 = 1.0 / r0
@@ -275,8 +290,10 @@
     sums0, sums1 = jnp.zeros((8, 256), F32), jnp.zeros((8, 256), F32)
     for rows in rows_of:
         part = z2[rows, :]
+        dh[rows, :], dl[rows, :] = split(part)
         sums0 = sums0 + fold8(z0[rows, :] * part)
         sums1 = sums1 + fold8(w1[rows, :] * part)
+    build_x()
     h01, h11 = total([sums0, sums1])
     h01, h11 = h01 * s0, h11 * s1
     f0, f1 = h01 * s0, h11 * s1
@@ -285,16 +302,21 @@
         part = z2[rows, :] - f0 * z0[rows, :] - f1 * w1[rows, :]
         if rows.start == 0:
             w2[...] = part[0:16]
-        dh[rows, :], dl[rows, :] = split(part)
         sums = sums + fold8(part * part)
-    build_x()
     h21 = jnp.sqrt(total([sums])[0])
     s2 = 1.0 / h21
-
-    last = apply_all() * s2
+    last = []
+    for half, part in enumerate(apply_all()):
+        some = slice(8 * half, 8 * half + 8)
+        last.append((part - h01 * z1[some, :] - h11 * z2[some, :]) * s2)
+    last = jnp.concatenate(last, axis=0)
+
     basis = [z0[0:16, :] * s0, w1[0:16, :] * s1, w2[...] * s2]
     sums = [jnp.sum(fold8(part * last), axis=0, keepdims=True) for part in basis + [last]]
-    pd[0] = jnp.concatenate([part[:, 128 * p : 128 * p + 128] for part in sums for p in range(2)], axis=0)
+    sums = segments(jnp.concatenate([part[:, 128 * p : 128 * p + 128] for part in sums for p in range(2)], axis=0))
+    lane8 = lax.broadcasted_iota(I32, (8, 128), 1)
+    eighth = (lane8 >> 3 & 7) == lax.broadcasted_iota(I32, (8, 128), 0)
+    pd[0] = jnp.sum(jnp.where(eighth, sums, 0.0), axis=0, keepdims=True)
     for dx, dy in peers_p:
         pltpu.make_async_remote_copy(
             src_ref=pd.at[0], dst_ref=pd.at[(-dx) % NX * NY + (-dy) % NY],
@@ -306,7 +328,8 @@
     c1, n1 = t1 * i1, h21 * i1
     g1, g2 = c1 * g1, -n1 * g1
     pltpu.make_async_copy(pd.at[pl.ds(1, 15)], pd.at[pl.ds(1, 15)], z_rx.at[3]).wait()
-    dots = segments(jnp.sum(pd[...], axis=0))
+    dots = jnp.broadcast_to(jnp.sum(pd[...], axis=0), (8, 128))
+    dots = segments(jnp.where(eighth & ((lane8 & 7) == 0), dots, 0.0))
     h02, h12, h22, zz = [jnp.concatenate([dots[2 * i : 2 * i + 1], dots[2 * i + 1 : 2 * i + 2]], axis=1) for i in range(4)]
     norm_sq = jnp.maximum(zz - h02 * h02 - h12 * h12 - h22 * h22, 0.0)
     u0, u1 = c0 * h02 + n0 * h12, c0 * h12 - n0 * h02
@@ -323,8 +346,6 @@
             device_id={"grp": in_grp(e, q), "sub": sub}, device_id_type=MESH,
         ).start()
     ob[grp] = sb[0]
-    for copy in sends:
-        copy.wait_send()
     pltpu.make_async_copy(pb.at[pl.ds(1, 15)], pb.at[pl.ds(1, 15)], b_tx).wait()
     for n, buf in enumerate((z0, z1, z2)):
         pltpu.make_async_copy(buf.at[pl.ds(16, 240)], buf.at[pl.ds(16, 240)], z_tx.at[n]).wait()
@@ -350,7 +371,7 @@
             pltpu.VMEM((1, 256), I32),
             pltpu.VMEM((8, 256), I32),
             pltpu.VMEM((64, 576), F32),
-            pltpu.VMEM((NZ, 2, CH, 72, 128), F32),
+            pltpu.VMEM((NZ, 2, CH, 32, 128), F32),
             pltpu.VMEM((4, 576, 256), BF16),
             pltpu.VMEM((4, 576, 256), BF16),
             pltpu.VMEM((16, 2, 128), F32),
@@ -363,15 +384,15 @@
             pltpu.VMEM((256, 256), BF16),
             pltpu.VMEM((256, 256), BF16),
             pltpu.VMEM((128, 256), BF16),
-            pltpu.VMEM((128, 576), BF16),
-            pltpu.VMEM((64, 256), F32),
-            pltpu.VMEM((16, 8, 128), F32),
+            pltpu.VMEM((2, 64, 576), BF16),
+            pltpu.VMEM((32, 256), F32),
+            pltpu.VMEM((16, 1, 128), F32),
             pltpu.VMEM((16, 2, 128), F32),
             pltpu.VMEM((16, 2, 128), F32),
-            dma((NZ, 2, CH)),
-            dma((4, CH)),
-            dma((4, CH)),
-            dma((NZ, CH)),
+            dma((NZ, 5)),
+            dma((CH,)),
+            dma((NZ,)),
+            dma,
             dma((4,)),
             dma,
             dma,

time: 55.1 us -> 52.7 us (0.956)
  Pallas kernels: 53.6 us -> 51.1 us
    pallas_call x1, Pallas kernels: 53.6 us -> 51.1 us  [per_device(): pl.pallas_call(kernel, out_shape=jax.ShapeDtypeStruct((1, 64, 64), F32),...]
where the time goes in v3:
time: 52.7 us; the launch traced here: 52.5 us
  Pallas kernels  51.1 us (97%)
  local copies, waits for them, and re-layouts  1.38 us (3%)
    pallas_call x1, Pallas kernels, per_device(): pl.pallas_call(kernel, out_shape=jax.ShapeDtypeStruct((1, 64, 64), F32),...  51.1 us
    unnamed x1, local copies, waits for them, and re-layouts  1.38 us

profile of v3, /device:TPU:1, one launch (start us, length us, event | category | flops | bytes accessed | tf_op | source)
XLA Modules:
  0.0 52.5 jit_solution(3769958339068245300)
XLA Ops:
  0.0 51.1 %shard_map.46 = f32[1,64,64]{2,1,0:T(8,128)} custom-call(f32[1,64,576]{2,1,0:T(8,128)} %op_hbm.1, f32[1,64,64]{2,1,0:T(8,128)} %b_hbm.1, s32[1,256]{1,0:T(1,128)} %bitcast.3, s32[8,256]{1,0:T(8,128)} %bitcast.2), custom_call_target="tpu_custom_call" | custom-call | tf_op jit(solution)/shard_map/pallas_call | solution.py:364
  51.1 1.4 %copy.6 = f32[1,64,64]{2,1,0:T(8,128)} copy(f32[1,64,64]{2,1,0:T(8,128)} %shard_map.46) | data formatting | bytes 32768
